TPU v7x, 32 devices: a whole 2x2x4 slice. The times are simulated.
32 devices in a mesh: band: 8 (over z, x), grid: 4 (over y, core).
Axes of the slice: x: 2, y: 2, z: 4, core: 2. Of those that a mesh axis runs over, the one named last changes fastest.
Arguments:
- partial_density: float32 [8, 128, 128, 128], P('band', 'grid'), may hold values from 0.01 to 1
- node_index: int32 [128, 128, 128], P('grid'), may hold values from 0 to 19
- node_weight: float32 [4, 128, 128, 128], P(None, 'grid'), may hold values from 0 to 1
- node_slope: float32 [4, 128, 128, 128], P(None, 'grid'), may hold values from -6 to 6
- kernel_table: float32 [20, 20, 114], replicated, may hold values from -0.8 to 0.8, as said below
Outputs:
- potential: float32 [128, 128, 128], P('grid')
Inputs may be any that keep to these rules, and one draw needn't show every extreme that they name: node_index(r) is the node at the lower end of the interval of q0 at r; nodes node_index - 1 to node_index + 2 carry the four weights. `kernel_table`: symmetric in its first two indices.
All inputs are finite; a program needn't handle non-finite values.
Results may differ from a plain program's by a relative error of at most 0.0003.
Values sent between devices are 32-bit elements; how exact they have to be, the bound alone decides.
A program may use at most 128 MiB of HBM per device.

v0:
```python
import math

import jax
import jax.numpy as jnp
from jax import lax
from jax.sharding import PartitionSpec as P

N = 128


def frequency_of(positions, length):
    return jnp.where(positions < length // 2, positions, positions - length)


def shell_split(square_norm):
    root_value = jnp.sqrt(square_norm.astype(jnp.float32))
    shell_idx = root_value.astype(jnp.int32)
    shell_idx = shell_idx - (shell_idx * shell_idx > square_norm).astype(jnp.int32)
    shell_idx = shell_idx + ((shell_idx + 1) * (shell_idx + 1) <= square_norm).astype(jnp.int32)
    fraction = root_value - shell_idx.astype(jnp.float32)
    return (shell_idx, fraction)


def node_fields(count_nodes, intervals, weights):
    node_ids = jnp.arange(count_nodes, dtype=jnp.int32)
    summed = jnp.zeros((count_nodes,) + intervals.shape, jnp.float32)
    for offset in range(4):
        matched = node_ids[:, None, None, None] == (intervals + (offset - 1))[None]
        summed = summed + jnp.where(matched, weights[offset][None], jnp.zeros((), jnp.float32))
    return summed


def phase_table(source_idx, target_idx, modulus):
    product_mod = source_idx[:, None] * target_idx[None, :] % modulus
    angles = product_mod.astype(jnp.float32) * (2.0 * math.pi / modulus)
    return (jnp.cos(angles), jnp.sin(angles))


def contract(pattern, operand, matrix):
    return jnp.einsum(pattern, operand, matrix, precision=lax.Precision.HIGHEST)


def mirrored(values, dim):
    return jnp.roll(jnp.flip(values, dim), 1, dim)


def forward_tables(positions, plane_ids, length):
    cosine, sine = phase_table(positions, plane_ids, length)
    alternating = jnp.where(positions % 2 == 0, 1.0, -1.0).astype(jnp.float32)
    sine = jnp.where(plane_ids[None, :] == 0, -alternating[:, None], sine)
    return (cosine, sine)


def shell_weights_of(square_norm, shell_count):
    shell_ids = jnp.arange(shell_count, dtype=jnp.int32)
    shell_idx, fraction = shell_split(square_norm)
    expand = (slice(None),) + (None,) * square_norm.ndim
    lower_hit = shell_ids[expand] == shell_idx[None]
    upper_hit = shell_ids[expand] == shell_idx[None] + 1
    return jnp.where(lower_hit, 1.0 - fraction[None], 0.0) + jnp.where(
        upper_hit, fraction[None], 0.0
    )


def per_device(partial_density, node_index, node_weight, node_slope, kernel_table):
    length = N
    half = length // 2
    count_nodes = kernel_table.shape[0]
    shell_count = kernel_table.shape[2]
    planes = half // lax.axis_size("band")
    grid_part = length // lax.axis_size("grid")
    band_at = lax.axis_index("band")
    grid_at = lax.axis_index("grid")
    full_range = jnp.arange(length, dtype=jnp.int32)
    own_planes = band_at * planes + jnp.arange(planes, dtype=jnp.int32)
    own_rows = grid_at * grid_part + jnp.arange(grid_part, dtype=jnp.int32)
    first_band = band_at == 0
    lower_rows = (full_range >= 1) & (full_range < half)
    upper_rows = full_range > half
    density = lax.psum(partial_density[0], "band")
    theta_fields = density[None] * node_fields(count_nodes, node_index, node_weight)
    cosine_z, sine_z = forward_tables(full_range, own_planes, length)
    forward_real = contract("axyz,zk->axyk", theta_fields, cosine_z)
    forward_imag = -contract("axyz,zk->axyk", theta_fields, sine_z)
    columns = jnp.stack([forward_real, forward_imag])
    cosine_full, sine_full = phase_table(full_range, full_range, length)
    y_cos = contract("caxyp,yw->caxpw", columns, cosine_full)
    y_sin = contract("caxyp,yw->caxpw", columns, sine_full)
    ywave_real = y_cos[0] + y_sin[1]
    ywave_imag = y_cos[1] - y_sin[0]
    first_real = ywave_real[:, :, 0, :]
    first_imag = ywave_imag[:, :, 0, :]
    turned_real = mirrored(first_real, 2)
    turned_imag = mirrored(first_imag, 2)
    packed_real = jnp.where(
        lower_rows,
        0.5 * (first_real + turned_real),
        jnp.where(upper_rows, 0.5 * (turned_imag + first_imag), first_real),
    )
    packed_imag = jnp.where(
        lower_rows,
        0.5 * (first_imag - turned_imag),
        jnp.where(upper_rows, 0.5 * (first_real - turned_real), first_imag),
    )
    ywave_real = ywave_real.at[:, :, 0, :].set(jnp.where(first_band, packed_real, first_real))
    ywave_imag = ywave_imag.at[:, :, 0, :].set(jnp.where(first_band, packed_imag, first_imag))
    pencils = lax.all_to_all(
        jnp.stack([ywave_real, ywave_imag]), "grid", split_axis=4, concat_axis=2, tiled=True
    )
    x_cos = contract("caxpw,xv->capwv", pencils, cosine_full)
    x_sin = contract("caxpw,xv->capwv", pencils, sine_full)
    spec_real = x_cos[0] + x_sin[1]
    spec_imag = x_cos[1] - x_sin[0]
    freq_x = frequency_of(full_range, length)
    square_x = freq_x * freq_x
    freq_rows = frequency_of(own_rows, length)
    plane_square = own_planes * own_planes
    third_square = jnp.where(
        (own_planes[:, None] == 0) & (own_rows[None, :] > half), half * half, plane_square[:, None]
    )
    special_rows = ((own_rows == 0) | (own_rows == half)) & (own_planes[0] == 0)

    def mix_row(row_idx):
        row_real = lax.dynamic_index_in_dim(spec_real, row_idx, 2, keepdims=False)
        row_imag = lax.dynamic_index_in_dim(spec_imag, row_idx, 2, keepdims=False)
        freq_row = lax.dynamic_index_in_dim(freq_rows, row_idx, 0, keepdims=False)
        third_row = lax.dynamic_index_in_dim(third_square, row_idx, 1, keepdims=False)
        square_norm = third_row[:, None] + square_x[None, :] + freq_row * freq_row
        kernel = contract("abs,spx->abpx", kernel_table, shell_weights_of(square_norm, shell_count))
        out_real = contract("abpx,apx->bpx", kernel, row_real)
        out_imag = contract("abpx,apx->bpx", kernel, row_imag)
        other_norm = square_x + freq_row * freq_row + half * half
        kernel_other = contract(
            "abs,sx->abx", kernel_table, shell_weights_of(other_norm, shell_count)
        )
        flag = lax.dynamic_index_in_dim(special_rows, row_idx, 0, keepdims=False).astype(
            jnp.float32
        )
        spread = 0.5 * flag * (kernel[:, :, 0, :] - kernel_other)
        base_real = row_real[:, 0, :]
        base_imag = row_imag[:, 0, :]
        delta_real = mirrored(base_real, 1) - base_real
        delta_imag = -mirrored(base_imag, 1) - base_imag
        out_real = out_real.at[:, 0, :].add(contract("abx,ax->bx", spread, delta_real))
        out_imag = out_imag.at[:, 0, :].add(contract("abx,ax->bx", spread, delta_imag))
        return jnp.stack([out_real, out_imag])

    mixed = lax.map(mix_row, jnp.arange(grid_part, dtype=jnp.int32))
    i_cos = contract("wcbpx,xv->wcbpv", mixed, cosine_full)
    i_sin = contract("wcbpx,xv->wcbpv", mixed, sine_full)
    inverse_real = i_cos[:, 0] - i_sin[:, 1]
    inverse_imag = i_cos[:, 1] + i_sin[:, 0]
    returned = lax.all_to_all(
        jnp.stack([inverse_real, inverse_imag], axis=1),
        "grid",
        split_axis=4,
        concat_axis=0,
        tiled=True,
    )
    lower_col = lower_rows[:, None, None]
    upper_col = upper_rows[:, None, None]
    back_real = returned[:, 0, :, 0, :]
    back_imag = returned[:, 1, :, 0, :]
    flip_real = mirrored(back_real, 0)
    flip_imag = mirrored(back_imag, 0)
    joined_real = jnp.where(
        lower_col, back_real - flip_imag, jnp.where(upper_col, flip_real + back_imag, back_real)
    )
    joined_imag = jnp.where(
        lower_col, back_imag + flip_real, jnp.where(upper_col, back_real - flip_imag, back_imag)
    )
    returned = returned.at[:, 0, :, 0, :].set(jnp.where(first_band, joined_real, back_real))
    returned = returned.at[:, 1, :, 0, :].set(jnp.where(first_band, joined_imag, back_imag))
    b_cos = contract("wcbpx,wy->cbpxy", returned, cosine_full)
    b_sin = contract("wcbpx,wy->cbpxy", returned, sine_full)
    slab_real = b_cos[0] - b_sin[1]
    slab_imag = b_cos[1] + b_sin[0]
    cosine_own, sine_own = phase_table(own_planes, full_range, length)
    alternating = jnp.where(full_range % 2 == 0, 1.0, -1.0).astype(jnp.float32)
    cosine_back = jnp.where(own_planes[:, None] == 0, 1.0, 2.0 * cosine_own)
    sine_back = jnp.where(own_planes[:, None] == 0, -alternating[None, :], 2.0 * sine_own)
    scale_factor = 1.0 / float(length) ** 3
    field_parts = (
        contract("bpxy,pz->bxyz", slab_real, cosine_back)
        - contract("bpxy,pz->bxyz", slab_imag, sine_back)
    ) * scale_factor
    slopes = node_fields(count_nodes, node_index, node_slope)
    partial_potential = jnp.sum(field_parts * slopes, axis=0)
    return lax.psum(partial_potential, "band")


def solution(mesh):
    placed = (
        P("band", "grid", None, None),
        P("grid", None, None),
        P(None, "grid", None, None),
        P(None, "grid", None, None),
        P(),
    )
    return jax.shard_map(
        per_device, mesh=mesh, in_specs=placed, out_specs=P("grid", None, None), check_vma=False
    )
```

profile of v0, /device:TPU:0, one launch (start us, length us, event | category | flops | bytes accessed | tf_op | source)
XLA Modules:
  0.0 1415.7 jit_solution(10311914120012794032)
XLA Ops:
  7.3 5.1 broadcast_add_fusion.4
  17.1 98.9 %all-reduce.3.cloned.1.call-done = f32[32,128,128]{2,1,0:T(8,128)} async-done(((f32[32,128,128]{2,1,0:T(8,128)}), f32[32,128,128]{2,1,0:T(8,128)}) %all-reduce.3.cloned.1.call-update) | async-done | bytes 2097168 | tf_op jit(solution)/shard_map/psum | solution.py:80
  116.0 66.0 %fusion.70 = f32[1,20,32,128,8]{3,4,2,1,0:T(8,128)} fusion(f32[32,128,128]{2,1,0:T(8,128)} %get-tuple-element.295, s32[32,128,128]{2,1,0:T(8,128)} %get-tuple-element.309, f32[32,128,128]{2,1,0:T(8,128)} %get-tuple-element.296, s32[32,128,128]{2,1,0:T(8,128)} %get-tuple-element.310, f32[32,128,128]{2,1,0:T(8,128)} %get-tuple-element.294, ...), kind=kOutput, calls=%fused_computation.132 | convolution fusion | flops 1132476416 | bytes 21495840 | tf_op jit(solution)/shard_map/axyz,zk->axyk/dot_general | solution.py:40
  182.0 57.5 %negate_bitcast_fusion = f32[1,20,32,128,8]{3,4,2,1,0:T(8,128)} fusion(f32[32,128,128]{2,1,0:T(8,128)} %get-tuple-element.295, s32[32,128,128]{2,1,0:T(8,128)} %get-tuple-element.309, f32[32,128,128]{2,1,0:T(8,128)} %get-tuple-element.296, s32[32,128,128]{2,1,0:T(8,128)} %get-tuple-element.310, f32[32,128,128]{2,1,0:T(8,128)} %get-tuple-element.294, ...), kind=kOutput, calls=%fused_computation.123 | convolution fusion | flops 1133132800 | bytes 21496360 | tf_op jit(solution)/shard_map/axyz,zk->axyk/dot_general | solution.py:40
  239.6 7.2 fusion.61
  246.8 4.7 fusion.62
  266.0 7.4 scatter.15
  273.4 9.3 scatter.14
  287.3 17.6 %copy.61 = f32[2,20,32,8,128]{2,3,1,0,4:T(8,128)} copy(f32[2,20,32,8,128]{4,3,2,1,0:T(8,128)} %pad_maximum_fusion.1) | data formatting | bytes 10485760 | tf_op jit(solution)/shard_map/stack | solution.py:108
  304.9 23.5 %reshape.667 = f32[4,1,327680]{2,1,0:T(1,128)} reshape(f32[128,2,20,8,32]{4,3,2,1,0:T(8,128)} %bitcast.306) | data formatting | bytes 10485760
  328.4 5.1 all-to-all-start
  333.6 59.3 %all-to-all-done = f32[4,1,327680]{2,1,0:T(1,128)} async-done(((f32[4,1,327680]{2,1,0:T(1,128)}), f32[4,1,327680]{2,1,0:T(1,128)}, u32[]{:S(2)}, u32[]{:S(2)}) %all-to-all-start) | async-done | bytes 5242912 | tf_op jit(solution)/shard_map/all_to_all | solution.py:107
  393.5 17.9 %reduce.21 = f32[4,327680]{1,0:T(4,128)} reduce(f32[4,1,327680]{2,1,0:T(1,128)} %all-to-all-done, f32[]{:T(128)} %broadcast.766), dimensions={1}, to_apply=%all_to_all.26.reduce_sub_computation | reduce | bytes 10485764 | tf_op jit(solution)/shard_map/all_to_all | solution.py:107
  411.4 16.7 %reshape.668 = f32[128,2,20,8,32]{4,3,2,1,0:T(8,128)} reshape(f32[4,327680]{1,0:T(4,128)} %reduce.21) | data formatting | bytes 10485760
  428.1 25.8 %copy.142 = f32[2,20,32,8,4,32]{2,4,5,3,1,0:T(4,128)} copy(f32[2,20,32,8,4,32]{2,3,1,0,5,4:T(8,128)} %bitcast.307) | data formatting | bytes 10485760 | tf_op jit(solution)/shard_map/all_to_all | solution.py:107
  453.9 16.5 %all_to_all.29 = f32[2,20,128,8,32]{2,4,3,1,0:T(8,128)} reshape(f32[2,20,4,32,8,32]{3,2,5,4,1,0:T(4,128)} %bitcast.308) | data formatting | bytes 10485760 | tf_op jit(solution)/shard_map/all_to_all | solution.py:107
  470.4 8.7 fusion.81
  486.7 425.2 %while.20 = (s32[]{:T(128)}, f32[32,2,20,8,128]{4,3,2,1,0:T(8,128)}, s32[32]{0:T(128)S(1)}, f32[20,8,32,128]{3,2,1,0:T(8,128)}, s32[8,32]{0,1:T(8,128)S(1)}, /*i...) while((s32[]{:T(128)}, ...), condition=%wide.region_2.3_spmd.clone.clone, body=%wide.region_1.2_spmd.clone.clone.sunk | while | flops 633025536 | bytes 4581378 | solution.py:148
  911.9 7.2 fusion.79
  927.4 17.5 %copy.63 = f32[32,2,20,8,128]{0,3,2,1,4:T(8,128)} copy(f32[32,2,20,8,128]{4,3,2,1,0:T(8,128)} %pad_maximum_fusion.2) | data formatting | bytes 10485760 | tf_op jit(solution)/shard_map/stack | solution.py:154
  945.0 23.5 %reshape.669 = f32[4,1,327680]{2,1,0:T(1,128)} reshape(f32[128,2,20,8,32]{4,3,2,1,0:T(8,128)} %bitcast.309) | data formatting | bytes 10485760
  968.5 5.1 all-to-all-start.1
  973.6 6.4 slice_bitcast_fusion.6
  979.9 53.0 %all-to-all-done.1 = f32[4,1,327680]{2,1,0:T(1,128)} async-done(((f32[4,1,327680]{2,1,0:T(1,128)}), f32[4,1,327680]{2,1,0:T(1,128)}, u32[]{:S(2)}, u32[]{:S(2)}) %all-to-all-start.1) | async-done | bytes 5242912 | tf_op jit(solution)/shard_map/all_to_all | solution.py:153
  1033.0 18.3 %reduce.22 = f32[4,327680]{1,0:T(4,128)} reduce(f32[4,1,327680]{2,1,0:T(1,128)} %all-to-all-done.1, f32[]{:T(128)} %broadcast.766), dimensions={1}, to_apply=%all_to_all.30.reduce_sub_computation | reduce | bytes 10485764 | tf_op jit(solution)/shard_map/all_to_all | solution.py:153
  1051.3 16.7 %reshape.670 = f32[128,2,20,8,32]{4,3,2,1,0:T(8,128)} reshape(f32[4,327680]{1,0:T(4,128)} %reduce.22) | data formatting | bytes 10485760
  1068.0 25.5 %copy.64 = f32[4,32,2,20,8,32]{1,0,5,3,4,2:T(4,128)} copy(f32[4,32,2,20,8,32]{1,4,3,2,5,0:T(8,128)} %bitcast.310) | data formatting | bytes 10485760 | tf_op jit(solution)/shard_map/all_to_all | solution.py:153
  1093.5 16.6 %all_to_all.33 = f32[128,2,20,8,32]{0,4,2,3,1:T(8,128)} reshape(f32[4,32,2,20,8,32]{1,0,5,3,4,2:T(4,128)} %copy.64) | data formatting | bytes 10485760 | tf_op jit(solution)/shard_map/all_to_all | solution.py:153
  1112.6 5.6 copy.175
  1138.9 69.8 %fusion.68 = f32[20,32,128,128]{3,2,1,0:T(8,128)} fusion(f32[20,8,32,128]{3,2,1,0:T(8,128)S(1)} %get-tuple-element.284, s32[8]{0:T(128)S(1)} %iota_add_fusion.1, pred[8]{0:T(512)(128)(4,1)S(1)} %broadcast_compare_fusion), kind=kOutput, calls=%fused_computation.121 | convolution fusion | flops 1006649344 | bytes 44564520 | tf_op jit(solution)/shard_map/bpxy,pz->bxyz/dot_general | solution.py:40
  1208.8 95.9 %multiply_reduce_fusion.4 = f32[32,128,128]{2,1,0:T(8,128)} fusion(f32[20,32,128,128]{3,2,1,0:T(8,128)} %fusion.68, f32[32,128,128]{2,1,0:T(8,128)S(1)} %copy-done.6, f32[32,128,128]{2,1,0:T(8,128)S(1)} %copy-done.7, f32[32,128,128]{2,1,0:T(8,128)S(1)} %copy-done.5, f32[32,128,128]{2,1,0:T(8,128)S(1)} %get-tuple-element.289, ...), kind=kOutput, calls=%fused_computation.74 | convolution fusion | flops 1163411456 | bytes 63439400 | tf_op jit(solution)/shard_map/bpxy,pz->bxyz/dot_general | solution.py:40
  1304.7 100.9 %all-reduce.5.cloned.1.call-done = f32[32,128,128]{2,1,0:T(8,128)} async-done(((f32[32,128,128]{2,1,0:T(8,128)}), f32[32,128,128]{2,1,0:T(8,128)}) %all-reduce.5.cloned.1.call-update) | async-done | bytes 2097168 | tf_op jit(solution)/shard_map/psum | solution.py:189
  (1133 shorter events, 363.7 us)
Async XLA Ops:
  6.5 109.5 %all-reduce.3.cloned.1.call-start = ((), (), s32[]{:S(2)}) async-start(), calls=%async_computation.2 | async-start | bytes 4194304 | tf_op jit(solution)/shard_map/psum | solution.py:80
  7.3 6.2 copy-start.12
  7.3 174.7 %copy-start.14 = (f32[128]{0:T(128)}, f32[128]{0:T(128)S(1)}, u32[]{:S(2)}) copy-start(f32[128]{0:T(128)S(1)} %fusion.141) | copy-start | bytes 1540
  13.5 102.5 %copy-start = (s32[32,128,128]{2,1,0:T(8,128)S(1)}, s32[32,128,128]{2,1,0:T(8,128)}, u32[]{:S(2)}) copy-start(s32[32,128,128]{2,1,0:T(8,128)} %param.20) | copy-start | bytes 6291460
  239.5 7.3 copy-start.10
  239.5 7.3 copy-start.11
  328.4 64.5 %all-to-all-start = ((f32[4,1,327680]{2,1,0:T(1,128)}), f32[4,1,327680]{2,1,0:T(1,128)}, u32[]{:S(2)}, u32[]{:S(2)}) async-start(f32[4,1,327680]{2,1,0:T(1,128)} %reshape.667), calls=%async_computation | async-start | bytes 10485760 | tf_op jit(solution)/shard_map/all_to_all | solution.py:107
  470.4 8.8 copy-start.8
  483.6 3.1 copy-start.13
  911.9 7.2 copy-start.9
  968.5 64.5 %all-to-all-start.1 = ((f32[4,1,327680]{2,1,0:T(1,128)}), f32[4,1,327680]{2,1,0:T(1,128)}, u32[]{:S(2)}, u32[]{:S(2)}) async-start(f32[4,1,327680]{2,1,0:T(1,128)} %reshape.669), calls=%async_computation.1 | async-start | bytes 10485760 | tf_op jit(solution)/shard_map/all_to_all | solution.py:153
  973.5 432.0 %all-reduce.5.cloned.1.call-start = ((), (), s32[]{:S(2)}) async-start(), calls=%async_computation.3 | async-start | bytes 4194304 | tf_op jit(solution)/shard_map/psum | solution.py:189
  1138.8 69.9 %copy-start.1 = (s32[32,128,128]{2,1,0:T(8,128)S(1)}, s32[32,128,128]{2,1,0:T(8,128)}, u32[]{:S(2)}) copy-start(s32[32,128,128]{2,1,0:T(8,128)} %param.20) | copy-start | bytes 6291460
  1138.8 69.9 %copy-start.2 = (s32[32,128,128]{2,1,0:T(8,128)S(1)}, s32[32,128,128]{2,1,0:T(8,128)}, u32[]{:S(2)}) copy-start(s32[32,128,128]{2,1,0:T(8,128)} %get-tuple-element.308) | copy-start | bytes 6291460
  1138.8 69.9 %copy-start.3 = (s32[32,128,128]{2,1,0:T(8,128)S(1)}, s32[32,128,128]{2,1,0:T(8,128)}, u32[]{:S(2)}) copy-start(s32[32,128,128]{2,1,0:T(8,128)} %get-tuple-element.309) | copy-start | bytes 6291460
  1138.8 69.9 %copy-start.4 = (s32[32,128,128]{2,1,0:T(8,128)S(1)}, s32[32,128,128]{2,1,0:T(8,128)}, u32[]{:S(2)}) copy-start(s32[32,128,128]{2,1,0:T(8,128)} %get-tuple-element.310) | copy-start | bytes 6291460
  1138.8 69.9 %copy-start.5 = (f32[32,128,128]{2,1,0:T(8,128)S(1)}, f32[32,128,128]{2,1,0:T(8,128)}, u32[]{:S(2)}) copy-start(f32[32,128,128]{2,1,0:T(8,128)} %get-tuple-element.290) | copy-start | bytes 6291460
  1138.8 69.9 %copy-start.6 = (f32[32,128,128]{2,1,0:T(8,128)S(1)}, f32[32,128,128]{2,1,0:T(8,128)}, u32[]{:S(2)}) copy-start(f32[32,128,128]{2,1,0:T(8,128)} %get-tuple-element.291) | copy-start | bytes 6291460
  1138.8 69.9 %copy-start.7 = (f32[32,128,128]{2,1,0:T(8,128)S(1)}, f32[32,128,128]{2,1,0:T(8,128)}, u32[]{:S(2)}) copy-start(f32[32,128,128]{2,1,0:T(8,128)} %get-tuple-element.292) | copy-start | bytes 6291460
  1138.8 69.9 %copy-start.15 = (f32[128]{0:T(128)S(1)}, f32[128]{0:T(128)}, u32[]{:S(2)}) copy-start(f32[128]{0:T(128)} %copy-done.14) | copy-start | bytes 1540
Sparse Core Ops, SparseCore 0:
  11.0 105.0 all-reduce.2
  1304.8 100.6 all-reduce.4
where the time goes:
time: 1430 us; the launch traced here: 1420 us
  matrix products  482 us (34%)
  local copies, waits for them, and re-layouts  368 us (26%)
  waiting for transfers between devices  313 us (22%)
  loops' own time  128 us (9%)
  other arithmetic  99.7 us (7%)
    dot_general x76, matrix products, contract(): return jnp.einsum(pattern, operand, matrix, precision=lax.Precision.HIGHEST)  482 us
    another operation x1, loops' own time, per_device(): mixed = lax.map(mix_row, jnp.arange(grid_part, dtype=jnp.int32))  128 us
    psum x1, waiting for transfers between devices, per_device(): return lax.psum(partial_potential, 'band')  101 us
    psum x1, waiting for transfers between devices, per_device(): density = lax.psum(partial_density[0], 'band')  98.9 us
    unnamed x39, local copies, waits for them, and re-layouts  92 us
    all_to_all x1, waiting for transfers between devices, per_device(): lax.all_to_all(jnp.stack([ywave_real, ywave_imag]), 'grid', split_axis=4,...  59.3 us
    all_to_all x1, waiting for transfers between devices, per_device(): lax.all_to_all(jnp.stack([inverse_real, inverse_imag], axis=1), 'grid', s...  53 us
    all_to_all x3, local copies, waits for them, and re-layouts, per_device(): lax.all_to_all(jnp.stack([ywave_real, ywave_imag]), 'grid', split_axis=4,...  42.8 us
  transfers between devices with their start and end apart: 4, of which 4 were waited for; matrix products, arithmetic and copies ran while one was open for 1% of the time, Pallas kernels for 0%

commit v1 on v0

v1 whole, which is shorter than its diff:
```python
import math

import jax
import jax.numpy as jnp
from jax import lax
from jax.experimental import pallas as pl
from jax.experimental.pallas import tpu as pltpu
from jax.sharding import PartitionSpec as P

def frequency_of(positions, length):
    return jnp.where(positions < length // 2, positions, positions - length)


def shell_split(square_norm):
    root_value = jnp.sqrt(square_norm.astype(jnp.float32))
    shell_idx = root_value.astype(jnp.int32)
    shell_idx = shell_idx - (shell_idx * shell_idx > square_norm).astype(jnp.int32)
    shell_idx = shell_idx + ((shell_idx + 1) * (shell_idx + 1) <= square_norm).astype(jnp.int32)
    fraction = root_value - shell_idx.astype(jnp.float32)
    return (shell_idx, fraction)


def node_fields(count_nodes, intervals, weights):
    node_ids = jnp.arange(count_nodes, dtype=jnp.int32)
    summed = jnp.zeros((count_nodes,) + intervals.shape, jnp.float32)
    for offset in range(4):
        matched = node_ids[:, None, None, None] == (intervals + (offset - 1))[None]
        summed = summed + jnp.where(matched, weights[offset][None], jnp.zeros((), jnp.float32))
    return summed


def phase_table(source_idx, target_idx, modulus):
    product_mod = source_idx[:, None] * target_idx[None, :] % modulus
    angles = product_mod.astype(jnp.float32) * (2.0 * math.pi / modulus)
    return (jnp.cos(angles), jnp.sin(angles))


def contract(pattern, operand, matrix):
    return jnp.einsum(pattern, operand, matrix, precision=lax.Precision.HIGHEST)


def mirrored(values, dim):
    return jnp.roll(jnp.flip(values, dim), 1, dim)


def forward_tables(positions, plane_ids, length):
    cosine, sine = phase_table(positions, plane_ids, length)
    alternating = jnp.where(positions % 2 == 0, 1.0, -1.0).astype(jnp.float32)
    sine = jnp.where(plane_ids[None, :] == 0, -alternating[:, None], sine)
    return (cosine, sine)


def shell_weights_of(square_norm, shell_count):
    shell_ids = jnp.arange(shell_count, dtype=jnp.int32)
    shell_idx, fraction = shell_split(square_norm)
    expand = (slice(None),) + (None,) * square_norm.ndim
    lower_hit = shell_ids[expand] == shell_idx[None]
    upper_hit = shell_ids[expand] == shell_idx[None] + 1
    return jnp.where(lower_hit, 1.0 - fraction[None], 0.0) + jnp.where(
        upper_hit, fraction[None], 0.0
    )


def short(pattern, left, right):
    return jnp.einsum(pattern, left, right, precision=lax.Precision.HIGH)


def halves(values):
    high = values.astype(jnp.bfloat16)
    low = (values - high.astype(jnp.float32)).astype(jnp.bfloat16)
    return high, low


def mix_kernel(count, padded, shell_ref, frac_ref, table_ref, spec_ref, out_ref):
    rows, lanes = shell_ref.shape[1:]
    ids = lax.broadcasted_iota(jnp.int32, (table_ref.shape[1] // 3, lanes), 0)

    def hats(row):
        shell = shell_ref[0, pl.ds(row, 1), :]
        frac = frac_ref[0, pl.ds(row, 1), :]
        return jnp.where(ids == shell, 1.0 - frac, jnp.where(ids == shell + 1, frac, 0.0))

    def step(pair, carry):
        both = jnp.concatenate([hats(2 * pair), hats(2 * pair + 1)], axis=1)
        high, low = halves(both)
        phi = jnp.dot(
            table_ref[...],
            jnp.concatenate([high, high, low], axis=0),
            preferred_element_type=jnp.float32,
        )
        for side in range(2):
            row = 2 * pair + side
            real = jnp.zeros((padded, lanes), jnp.float32)
            imag = jnp.zeros((padded, lanes), jnp.float32)
            for node in range(count):
                part = phi[node * padded : (node + 1) * padded, side * lanes : (side + 1) * lanes]
                real = real + part * spec_ref[0, node, 0, pl.ds(row, 1), :]
                imag = imag + part * spec_ref[1, node, 0, pl.ds(row, 1), :]
            out_ref[0, row, 0] = real[:count]
            out_ref[0, row, 1] = imag[:count]
        return carry

    lax.fori_loop(0, rows // 2, step, 0)


def mix(spectrum, shell, frac, kernel_table):
    _, count, planes, rows, lanes = spectrum.shape
    padded = -(-count // 8) * 8
    depth = -(-(kernel_table.shape[2]) // 128) * 128
    table = jnp.pad(kernel_table, ((0, 0), (0, padded - count), (0, depth - kernel_table.shape[2])))
    table = table.reshape(count * padded, depth)
    rounded = lax.reduce_precision(table, exponent_bits=8, mantissa_bits=7)
    high, low = rounded.astype(jnp.bfloat16), (table - rounded).astype(jnp.bfloat16)
    table = jnp.concatenate([high, low, high], axis=1)
    return pl.pallas_call(
        lambda *refs: mix_kernel(count, padded, *refs),
        grid=(planes,),
        in_specs=[
            pl.BlockSpec((1, rows, lanes), lambda p: (p, 0, 0)),
            pl.BlockSpec((1, rows, lanes), lambda p: (p, 0, 0)),
            pl.BlockSpec(table.shape, lambda p: (0, 0)),
            pl.BlockSpec((2, count, 1, rows, lanes), lambda p: (0, 0, p, 0, 0)),
        ],
        out_specs=pl.BlockSpec((1, rows, 2, count, lanes), lambda p: (p, 0, 0, 0, 0)),
        out_shape=jax.ShapeDtypeStruct((planes, rows, 2, count, lanes), jnp.float32),
    )(shell, frac, table, spectrum)


def per_device(partial_density, node_index, node_weight, node_slope, kernel_table):
    length = node_index.shape[1]
    half = length // 2
    count_nodes = kernel_table.shape[0]
    shell_count = kernel_table.shape[2]
    planes = half // lax.axis_size("band")
    grid_size = lax.axis_size("grid")
    grid_part = length // grid_size
    band_at = lax.axis_index("band")
    grid_at = lax.axis_index("grid")
    full_range = jnp.arange(length, dtype=jnp.int32)
    own_planes = band_at * planes + jnp.arange(planes, dtype=jnp.int32)
    own_rows = grid_at * grid_part + jnp.arange(grid_part, dtype=jnp.int32)
    lower = ((full_range >= 1) & (full_range < half)).astype(jnp.float32)
    upper = (full_range > half).astype(jnp.float32)
    single = 1.0 - lower - upper
    joint = (own_planes == 0)[:, None, None, None, None]
    cosine, sine = phase_table(full_range, full_range, length)
    forward = jnp.stack(
        [jnp.stack([cosine, -sine], 1), jnp.stack([sine, cosine], 1)]
    )
    low_only = lower + single
    packed = jnp.stack(
        [
            jnp.stack([cosine * low_only, -sine * lower], 1),
            jnp.stack([cosine * upper, -sine * upper + cosine * single], 1),
        ]
    )
    forward_y = jnp.where(joint, packed[None], forward[None])
    backward = jnp.stack(
        [jnp.stack([cosine, sine], 1), jnp.stack([-sine, cosine], 1)]
    )
    lower_col, upper_col, single_col = (v[:, None] for v in (lower, upper, single))
    opened = jnp.stack(
        [
            jnp.stack([cosine * (2.0 * lower_col + single_col), cosine * (2.0 * upper_col)], 1),
            jnp.stack(
                [sine * (-2.0 * lower_col), sine * (-2.0 * upper_col) + cosine * single_col], 1
            ),
        ]
    )
    backward_y = jnp.where(joint, opened[None], backward[None])

    density = lax.psum(partial_density[0], "band")
    theta_fields = density[None] * node_fields(count_nodes, node_index, node_weight)
    cosine_z, sine_z = forward_tables(full_range, own_planes, length)
    table_z = jnp.stack([cosine_z, -sine_z], 1)
    columns = short("zcp,axyz->cpaxy", table_z, theta_fields)
    waves = short("cpaxy,pcydw->wdapx", columns, forward_y)
    waves = waves.reshape((grid_size, grid_part) + waves.shape[1:])
    pencils = lax.all_to_all(waves, "grid", split_axis=0, concat_axis=0, tiled=True)
    forward_x = forward.reshape((2, grid_size, grid_part) + forward.shape[2:])
    spectrum = short("gwdapx,dgxev->eapwv", pencils, forward_x)

    freq_x = frequency_of(full_range, length)
    square_x = freq_x * freq_x
    freq_rows = frequency_of(own_rows, length)
    square_rows = freq_rows * freq_rows
    third_square = jnp.where(
        (own_planes[:, None] == 0) & (own_rows[None, :] > half),
        half * half,
        (own_planes * own_planes)[:, None],
    )
    square_norm = (third_square + square_rows[None, :])[:, :, None] + square_x
    shell, frac = shell_split(square_norm)
    mixed = mix(spectrum, shell, frac, kernel_table)

    flag = ((own_rows[0] == 0) | (own_rows[0] == half)) & (own_planes[0] == 0)
    first_norm = square_x + square_rows[0]
    pair_norm = jnp.stack([first_norm, first_norm + half * half])
    kernels = contract("abs,sqx->qabx", kernel_table, shell_weights_of(pair_norm, shell_count))
    spread = (0.5 * flag.astype(jnp.float32)) * (kernels[0] - kernels[1])
    base = spectrum[:, :, 0, 0, :]
    turned = mirrored(base, 2)
    delta = jnp.stack([turned[0] - base[0], -turned[1] - base[1]])
    extra = jnp.sum(spread[None] * delta[:, :, None, :], axis=1)
    mixed = mixed.at[0, 0].add(extra)

    backward_x = backward.reshape(2, length, 2, grid_size, grid_part)
    inverse = short("pwdbv,dvegx->gwebpx", mixed, backward_x)
    returned = lax.all_to_all(inverse, "grid", split_axis=0, concat_axis=0, tiled=True)
    backward_y = backward_y.reshape((planes, 2, grid_size, grid_part, 2, length))
    slab = short("gwdbpx,pdgwcy->cpbxy", returned, backward_y)
    cosine_own, sine_own = phase_table(own_planes, full_range, length)
    alternating = jnp.where(full_range % 2 == 0, 1.0, -1.0).astype(jnp.float32)
    cosine_back = jnp.where(own_planes[:, None] == 0, 1.0, 2.0 * cosine_own)
    sine_back = jnp.where(own_planes[:, None] == 0, -alternating[None, :], 2.0 * sine_own)
    table_back = jnp.stack([cosine_back, -sine_back]) * (1.0 / float(length) ** 3)
    field_parts = short("cpbxy,cpz->bxyz", slab, table_back)
    slopes = node_fields(count_nodes, node_index, node_slope)
    partial_potential = jnp.sum(field_parts * slopes, axis=0)
    return lax.psum(partial_potential, "band")


def solution(mesh):
    placed = (
        P("band", "grid", None, None),
        P("grid", None, None),
        P(None, "grid", None, None),
        P(None, "grid", None, None),
        P(),
    )
    return jax.shard_map(
        per_device, mesh=mesh, in_specs=placed, out_specs=P("grid", None, None), check_vma=False
    )
```

time: 1430 us -> 761 us (0.53)
  matrix products: 482 us -> 161 us
  local copies, waits for them, and re-layouts: 368 us -> 158 us
  loops' own time: 128 us -> 0 us
  other arithmetic: 99.7 us -> 46.6 us
  Pallas kernels: 0 us -> 40.6 us
    dot_general x76 -> x1, matrix products: 482 us -> 0.58 us  [contract(): return jnp.einsum(pattern, operand, matrix, precision=lax.Precision.HIGHEST)]
    dot_general x0 -> x6, matrix products: none -> 161 us  [short(): return jnp.einsum(pattern, left, right, precision=lax.Precision.HIGH)]
    another operation x1 -> x0, loops' own time: 128 us -> none  [per_device(): mixed = lax.map(mix_row, jnp.arange(grid_part, dtype=jnp.int32))]
    dynamic_slice x128 -> x0, local copies, waits for them, and re-layouts: 96.4 us -> none  [the longest x32 39.2 us: mix_row(): row_imag = lax.dynamic_index_in_dim(spec_imag, row_idx, 2, keepdims=False)]
    all_to_all x5 -> x1, local copies, waits for them, and re-layouts: 85 us -> 0.58 us  [per_device(): lax.all_to_all(waves, 'grid', split_axis=0, concat_axis=0, tiled=True)]
    pallas_call x0 -> x1, Pallas kernels: none -> 40.6 us  [mix(): pl.pallas_call(lambda *refs: mix_kernel(count, padded, *refs), grid=(plan...]
    reshape x0 -> x2, local copies, waits for them, and re-layouts: none -> 39.4 us  [per_device(): waves = waves.reshape((grid_size, grid_part) + waves.shape[1:])]
    another operation x2 -> x0, local copies, waits for them, and re-layouts: 35.2 us -> none  [the longest x1 17.6 us: per_device(): jnp.stack([ywave_real, ywave_imag])]
  transfers between devices with their start and end apart: 4 -> 4, of which waited for: 4 -> 4; matrix products, arithmetic and copies ran while one was open for 1% -> 3% of each run, Pallas kernels for 0% -> 0%
where the time goes in v1:
time: 761 us; the launch traced here: 751 us
  waiting for transfers between devices  308 us (40%)
  matrix products  161 us (21%)
  local copies, waits for them, and re-layouts  158 us (21%)
  other arithmetic  46.6 us (6%)
  Pallas kernels  40.6 us (5%)
  starting transfers between devices  21.4 us (3%)
  between operations  14.1 us (2%)
    dot_general x6, matrix products, short(): return jnp.einsum(pattern, left, right, precision=lax.Precision.HIGH)  161 us
    psum x1, waiting for transfers between devices, per_device(): return lax.psum(partial_potential, 'band')  101 us
    psum x1, waiting for transfers between devices, per_device(): density = lax.psum(partial_density[0], 'band')  100 us
    unnamed x20, local copies, waits for them, and re-layouts  86.5 us
    all_to_all x1, waiting for transfers between devices, per_device(): lax.all_to_all(waves, 'grid', split_axis=0, concat_axis=0, tiled=True)  54.8 us
    all_to_all x1, waiting for transfers between devices, per_device(): lax.all_to_all(inverse, 'grid', split_axis=0, concat_axis=0, tiled=True)  52.1 us
    pallas_call x1, Pallas kernels, mix(): pl.pallas_call(lambda *refs: mix_kernel(count, padded, *refs), grid=(plan...  40.6 us
    reshape x2, local copies, waits for them, and re-layouts, per_device(): waves = waves.reshape((grid_size, grid_part) + waves.shape[1:])  39.4 us
  transfers between devices with their start and end apart: 4, of which 4 were waited for; matrix products, arithmetic and copies ran while one was open for 3% of the time, Pallas kernels for 0%

profile of v1, /device:TPU:0, one launch (start us, length us, event | category | flops | bytes accessed | tf_op | source)
XLA Modules:
  0.0 750.6 jit_solution(15653981110565317054)
XLA Ops:
  8.7 3.1 broadcast_add_fusion.2
  12.5 3.5 slice_bitcast_fusion.7
  16.0 100.0 %all-reduce.4.cloned.1.call-done = f32[32,128,128]{2,1,0:T(8,128)} async-done(((f32[32,128,128]{2,1,0:T(8,128)}), f32[32,128,128]{2,1,0:T(8,128)}) %all-reduce.4.cloned.1.call-update) | async-done | bytes 2097168 | tf_op jit(solution)/shard_map/psum | solution.py:172
  116.0 35.8 %fusion.39 = f32[2,8,20,32,128,1]{4,1,3,2,0,5:T(8,128)S(1)} fusion(f32[32,128,128]{2,1,0:T(8,128)} %get-tuple-element.22, s32[32,128,128]{2,1,0:T(8,128)} %get-tuple-element.31, f32[32,128,128]{2,1,0:T(8,128)} %get-tuple-element.23, s32[32,128,128]{2,1,0:T(8,128)} %get-tuple-element.32, f32[32,128,128]{2,1,0:T(8,128)} %get-tuple-element.21, ...), kind=kOutput, calls=%fused_computation.39 | convolution fusion | flops 1132464128 | bytes 24125440 | tf_op jit(solution)/shard_map/zcp,axyz->cpaxy/dot_general | solution.py:65
  151.8 5.0 fusion.30
  156.8 15.4 %reshape.1184 = f32[4,32,2,20,8,32]{1,0,5,3,2,4:T(4,128)} reshape(f32[128,2,20,8,32]{0,4,2,1,3:T(8,128)} %fusion.30) | data formatting | bytes 10485760 | tf_op jit(solution)/shard_map/reshape | solution.py:178
  172.2 24.0 %copy.26 = f32[4,32,2,20,8,32]{5,1,2,4,3,0:T(8,128)} copy(f32[4,32,2,20,8,32]{1,0,5,3,2,4:T(4,128)} %reshape.1184) | data formatting | bytes 10485760 | tf_op jit(solution)/shard_map/reshape | solution.py:178
  196.2 23.5 %reshape.1204 = f32[4,1,327680]{2,1,0:T(1,128)} reshape(f32[4,20,8,2,32,32]{5,4,3,2,1,0:T(8,128)} %bitcast.148) | data formatting | bytes 10485760
  219.7 16.2 %all-to-all-start = ((f32[4,1,327680]{2,1,0:T(1,128)}), f32[4,1,327680]{2,1,0:T(1,128)}, u32[]{:S(2)}, u32[]{:S(2)}) async-start(f32[4,1,327680]{2,1,0:T(1,128)} %reshape.1204), calls=%async_computation | async-start | bytes 10485760 | tf_op jit(solution)/shard_map/all_to_all | solution.py:179
  236.3 0.8 pad_maximum_fusion.refs_2_
  237.2 0.8 convert_add_fusion.refs_0_
  238.0 0.8 fusion.64.refs_1_
  240.2 54.8 %all-to-all-done = f32[4,1,327680]{2,1,0:T(1,128)} async-done(((f32[4,1,327680]{2,1,0:T(1,128)}), f32[4,1,327680]{2,1,0:T(1,128)}, u32[]{:S(2)}, u32[]{:S(2)}) %all-to-all-start) | async-done | bytes 5242912 | tf_op jit(solution)/shard_map/all_to_all | solution.py:179
  295.6 17.9 %reduce.2 = f32[4,327680]{1,0:T(4,128)} reduce(f32[4,1,327680]{2,1,0:T(1,128)} %all-to-all-done, f32[]{:T(128)} %broadcast.1674), dimensions={1}, to_apply=%all_to_all.6.reduce_sub_computation | reduce | bytes 10485764 | tf_op jit(solution)/shard_map/all_to_all | solution.py:179
  313.5 16.7 %reshape.1205 = f32[4,20,8,2,32,32]{5,4,3,2,1,0:T(8,128)} reshape(f32[4,327680]{1,0:T(4,128)} %reduce.2) | data formatting | bytes 10485760
  330.2 16.0 %fusion.33.refs_3_ = f32[2,20,8,32,128]{4,3,2,1,0:T(8,128)S(1)} fusion(f32[1,4,32,1,128]{4,2,1,0,3:T(8,128)S(1)} %get-tuple-element.43, f32[1,4,32,1,128]{4,2,1,0,3:T(8,128)S(1)} %get-tuple-element.40, f32[1,4,32,1,128]{4,2,1,0,3:T(8,128)S(1)} %get-tuple-element.42, f32[4,20,8,2,32,32]{5,4,3,2,1,0:T(8,128)} %reshape.1205), kind=kOutput, calls=%fused_computation.37 | convolution fusion | flops 2013462528 | bytes 10682368 | tf_op jit(solution)/shard_map/gwdapx,dgxev->eapwv/dot_general | solution.py:65
  346.2 2.3 copy-done.2
  348.8 1.0 fusion.106
  350.0 40.6 %shard_map.55 = f32[8,32,2,20,128]{4,3,2,1,0:T(8,128)} custom-call(s32[8,32,128]{2,1,0:T(8,128)} %convert_add_fusion.refs_0_, f32[8,32,128]{2,1,0:T(8,128)} %fusion.64.refs_1_, bf16[480,384]{1,0:T(8,128)(2,1)} %pad_maximum_fusion.refs_2_, f32[2,20,8,32,128]{4,3,2,1,0:T(8,128)} %copy-done.2), custom_call_target="tpu_custom_call" | custom-call | tf_op jit(solution)/shard_map/pallas_call | solution.py:115
  390.7 1.3 fusion.103
  392.0 13.3 %convolution_bitcast_fusion = f32[4,32,2,20,8,32]{1,5,3,4,0,2:T(8,128)} fusion(f32[8,32,2,20,128,1,1]{4,3,2,1,0,6,5:T(8,128)} %bitcast.149, f32[1,128,1,4,32]{1,4,3,2,0:T(8,128)S(1)} %get-tuple-element.45, f32[1,128,1,4,32]{1,4,3,2,0:T(8,128)S(1)} %get-tuple-element.46, f32[1,128,1,4,32]{1,4,3,2,0:T(8,128)S(1)} %get-tuple-element.44), kind=kOutput, calls=%fused_computation.31 | convolution fusion | flops 2013462528 | bytes 10682368 | tf_op jit(solution)/shard_map/pwdbv,dvegx->gwebpx/dot_general | solution.py:65
  405.3 20.8 %copy.33 = f32[4,32,2,20,8,32]{5,4,3,2,1,0:T(8,128)} copy(f32[4,32,2,20,8,32]{1,5,3,4,0,2:T(8,128)} %convolution_bitcast_fusion) | data formatting | bytes 10485760 | tf_op jit(solution)/shard_map/pwdbv,dvegx->gwebpx/transpose | solution.py:65
  426.1 23.5 %reshape.1206 = f32[4,1,327680]{2,1,0:T(1,128)} reshape(f32[4,32,2,20,8,32]{5,4,3,2,1,0:T(8,128)} %copy.33) | data formatting | bytes 10485760
  449.5 5.2 all-to-all-start.1
  455.0 7.1 slice_bitcast_fusion.3
  462.1 52.1 %all-to-all-done.1 = f32[4,1,327680]{2,1,0:T(1,128)} async-done(((f32[4,1,327680]{2,1,0:T(1,128)}), f32[4,1,327680]{2,1,0:T(1,128)}, u32[]{:S(2)}, u32[]{:S(2)}) %all-to-all-start.1) | async-done | bytes 5242912 | tf_op jit(solution)/shard_map/all_to_all | solution.py:209
  514.2 18.0 %reduce.3 = f32[4,327680]{1,0:T(4,128)} reduce(f32[4,1,327680]{2,1,0:T(1,128)} %all-to-all-done.1, f32[]{:T(128)} %broadcast.1674), dimensions={1}, to_apply=%all_to_all.7.reduce_sub_computation | reduce | bytes 10485764 | tf_op jit(solution)/shard_map/all_to_all | solution.py:209
  532.2 16.7 %reshape.1207 = f32[4,32,2,20,8,32]{5,4,3,2,1,0:T(8,128)} reshape(f32[4,327680]{1,0:T(4,128)} %reduce.3) | data formatting | bytes 10485760
  548.9 34.4 %fusion.36 = f32[2,8,20,32,128]{4,3,2,0,1:T(8,128)} fusion(f32[4,32,2,20,8,32,1]{5,4,3,2,1,0,6:T(8,128)} %bitcast.147, f32[2,4,32,2,128]{4,2,1,0,3:T(8,128)S(1)} %get-tuple-element.61, f32[2,4,32,2,128]{4,2,1,0,3:T(8,128)S(1)} %get-tuple-element.62, pred[8]{0:T(512)(128)(4,1)S(1)} %broadcast_compare_fusion.1), kind=kOutput, calls=%fused_computation.38 | convolution fusion | flops 2013790208 | bytes 11010056 | tf_op jit(solution)/shard_map/gwdbpx,pdgwcy->cpbxy/dot_general | solution.py:65
  583.4 56.2 %fusion = f32[32,128,128]{2,1,0:T(8,128)} fusion(f32[32,128,128]{2,1,0:T(8,128)} %get-tuple-element.26, f32[32,128,128]{2,1,0:T(8,128)} %get-tuple-element.27, f32[32,128,128]{2,1,0:T(8,128)} %get-tuple-element.25, f32[32,128,128]{2,1,0:T(8,128)} %get-tuple-element.24, s32[32,128,128]{2,1,0:T(8,128)} %get-tuple-element.31, ...), kind=kOutput, calls=%fused_computation.1 | convolution fusion | flops 1142423552 | bytes 24125440 | tf_op jit(solution)/shard_map/cpbxy,cpz->bxyz/dot_general | solution.py:65
  639.6 100.8 %all-reduce.6.cloned.1.call-done = f32[32,128,128]{2,1,0:T(8,128)} async-done(((f32[32,128,128]{2,1,0:T(8,128)}), f32[32,128,128]{2,1,0:T(8,128)}) %all-reduce.6.cloned.1.call-update) | async-done | bytes 2097168 | tf_op jit(solution)/shard_map/psum | solution.py:220
  740.4 3.1 copy.92
  (63 shorter events, 5.6 us)
Async XLA Ops:
  6.5 2.2 copy-start
  6.5 109.5 %all-reduce.4.cloned.1.call-start = ((), (), s32[]{:S(2)}) async-start(), calls=%async_computation.2 | async-start | bytes 4194304 | tf_op jit(solution)/shard_map/psum | solution.py:172
  7.3 5.2 copy-start.3
  7.3 8.7 %copy-start.5 = (f32[128]{0:T(128)}, f32[128]{0:T(128)S(1)}, u32[]{:S(2)}) copy-start(f32[128]{0:T(128)S(1)} %fusion.134) | copy-start | bytes 1540
  219.6 16.4 %copy-start.4 = (f32[20,20,114]{2,1,0:T(8,128)S(1)}, f32[20,20,114]{2,1,0:T(8,128)}, u32[]{:S(2)}) copy-start(f32[20,20,114]{2,1,0:T(8,128)} %param.11) | copy-start | bytes 547204
  219.7 75.4 %all-to-all-start = ((f32[4,1,327680]{2,1,0:T(1,128)}), f32[4,1,327680]{2,1,0:T(1,128)}, u32[]{:S(2)}, u32[]{:S(2)}) async-start(f32[4,1,327680]{2,1,0:T(1,128)} %reshape.1204), calls=%async_computation | async-start | bytes 10485760 | tf_op jit(solution)/shard_map/all_to_all | solution.py:179
  346.2 2.3 copy-start.2
  449.5 5.2 copy-start.6
  449.5 64.6 %all-to-all-start.1 = ((f32[4,1,327680]{2,1,0:T(1,128)}), f32[4,1,327680]{2,1,0:T(1,128)}, u32[]{:S(2)}, u32[]{:S(2)}) async-start(f32[4,1,327680]{2,1,0:T(1,128)} %reshape.1206), calls=%async_computation.1 | async-start | bytes 10485760 | tf_op jit(solution)/shard_map/all_to_all | solution.py:209
  454.7 285.7 %all-reduce.6.cloned.1.call-start = ((), (), s32[]{:S(2)}) async-start(), calls=%async_computation.3 | async-start | bytes 4194304 | tf_op jit(solution)/shard_map/psum | solution.py:220
  548.9 34.4 %copy-start.1 = (s32[32,128,128]{2,1,0:T(8,128)S(1)}, s32[32,128,128]{2,1,0:T(8,128)}, u32[]{:S(2)}) copy-start(s32[32,128,128]{2,1,0:T(8,128)} %get-tuple-element.30) | copy-start | bytes 6291460
Sparse Core Ops, SparseCore 0:
  11.0 105.0 all-reduce.3
  639.7 100.6 all-reduce.5
